TPU v7x, 32 devices: a whole 2x2x4 slice. The times are simulated.
32 devices in a mesh: expert: 8 (over y, x, core), dp: 4 (over z).
Axes of the slice: x: 2, y: 2, z: 4, core: 2. Of those that a mesh axis runs over, the one named last changes fastest.
Arguments:
- gradient: bfloat16 [4, 1, 14336, 2048], P('dp', None, None, 'expert'), may hold values from -6 to 6
- momentum: float32 [4, 1, 14336, 2048], P('dp', None, 'expert'), may hold values from -6 to 6
- group_index: int32 [224, 32, 4, 32], P('expert'), may hold values from 0 to 4095, all different within a row
Outputs:
- momentum_next: float32 [4, 1, 14336, 2048], P('dp', None, 'expert')
- update: float32 [1, 14336, 2048], P(None, None, 'expert')
Inputs may be any that keep to these rules, and one draw needn't show every extreme that they name: `group_index`: an entry names the coefficient at row frequency (entry // 64) and column frequency (entry % 64) of its block; the 32 entries of one block and replica differ.
All inputs are finite; a program needn't handle non-finite values.
Results may differ from a plain program's by a relative error of at most 0.0003.
Values may be sent and summed in bfloat16 or wider, within the bound.
No kernel may reach another device: no remote copies, remote signals or barrier semaphores. Data moves between devices by JAX's collectives and lax.ppermute only.
A program may use at most 192 MiB of HBM per device.

v0:
```python
import math
import jax
import jax.numpy as jnp
from jax import lax
from jax.sharding import PartitionSpec as P

SPAN = 64
MOMENTUM_DECAY = 0.999
HIGHEST_PRECISION = lax.Precision.HIGHEST


def cosine_table(order_size):
    frequency = jnp.arange(order_size, dtype=jnp.float32)[:, None]
    position = jnp.arange(order_size, dtype=jnp.float32)[None, :]
    weighting = jnp.where(frequency == 0, math.sqrt(1.0 / order_size), math.sqrt(2.0 / order_size))
    return weighting * jnp.cos(math.pi * (2.0 * position + 1.0) * frequency / (2.0 * order_size))


def forward(blocks, cosine):
    return jnp.einsum("ui,piqj,vj->pquv", cosine, blocks, cosine, precision=HIGHEST_PRECISION)


def inverse(coeffs, cosine):
    return jnp.einsum("ui,pquv,vj->piqj", cosine, coeffs, cosine, precision=HIGHEST_PRECISION)


def place(values, picked, total):
    count_rows = picked.shape[0]
    count_cols = picked.shape[1]
    row_ids = jnp.arange(count_rows, dtype=jnp.int32)[:, None, None]
    col_ids = jnp.arange(count_cols, dtype=jnp.int32)[None, :, None]
    empty = jnp.zeros((count_rows, count_cols, total), jnp.float32)
    return empty.at[row_ids, col_ids, picked].add(values)


def on_device(gradient, momentum, group_index):
    cosine = cosine_table(SPAN)
    replica = lax.axis_index("dp")
    shifted = lax.all_to_all(gradient, "expert", split_axis=2, concat_axis=3, tiled=True)
    row_count = shifted.shape[1] * shifted.shape[2]
    col_count = shifted.shape[3]
    decayed = MOMENTUM_DECAY * momentum.reshape(row_count, col_count) + shifted.reshape(
        row_count, col_count
    ).astype(jnp.float32)
    block_rows = row_count // SPAN
    block_cols = col_count // SPAN
    blocks = decayed.reshape(block_rows, SPAN, block_cols, SPAN)
    coeffs = forward(blocks, cosine).reshape(block_rows, block_cols, SPAN * SPAN)
    own = lax.dynamic_index_in_dim(group_index, replica, 2, keepdims=False)
    values = jnp.take_along_axis(coeffs, own, axis=2)
    selected = place(values, own, SPAN * SPAN).reshape(block_rows, block_cols, SPAN, SPAN)
    restored = inverse(selected, cosine).reshape(row_count, col_count)
    momentum_next = (decayed - restored).reshape(momentum.shape)
    total = lax.psum(restored, "dp")
    update = lax.all_to_all(total[None], "expert", split_axis=2, concat_axis=1, tiled=True)
    return (momentum_next, update)


def solution(mesh):
    placed = (
        P("dp", None, None, "expert"),
        P("dp", None, "expert", None),
        P("expert", None, None, None),
    )
    return jax.shard_map(
        on_device,
        mesh=mesh,
        in_specs=placed,
        out_specs=(P("dp", None, "expert", None), P(None, None, "expert")),
        check_vma=False,
    )
```

profile of v0, /device:TPU:0, one launch (start us, length us, event | category | flops | bytes accessed | tf_op | source)
XLA Modules:
  0.0 1791.6 jit_solution(7726705985942069426)
XLA Ops:
  7.2 13.9 copy.47
  21.6 74.4 %reduce.4 = bf16[14336,256]{1,0:T(8,128)(2,1)} reduce(bf16[14336,1,1,256]{3,2,1,0:T(2,128)(2,1)} %bitcast.50, bf16[]{:T(256)} %broadcast.103), dimensions={1,2}, to_apply=%bitcast.46.reduce_sub_computation | reduce | bytes 14680066
  96.0 9.0 reshape.130
  105.1 5.2 all-to-all-start
  111.4 0.8 copy-done.2
  113.1 0.8 reshape.121
  113.9 14.1 broadcast_multiply_fusion
  128.0 24.3 %mul.98 = f32[28,64,32,64]{3,2,1,0:T(8,128)} reshape(f32[1,1,1792,2048]{3,2,1,0:T(8,128)} %broadcast_multiply_fusion) | data formatting | bytes 29360128 | tf_op jit(solution)/shard_map/mul | solution.py:42
  152.5 40.9 %all-to-all-done = bf16[8,2,229376]{2,1,0:T(2,128)(2,1)} async-done(((bf16[8,2,229376]{2,1,0:T(2,128)(2,1)}), bf16[8,2,229376]{2,1,0:T(2,128)(2,1)}, u32[]{:S(2)}, u32[]{:S(2)}) %all-to-all-start) | async-done | bytes 7340064 | tf_op jit(solution)/shard_map/all_to_all | solution.py:39
  193.4 12.1 reshape.131
  205.5 15.9 copy.46
  221.4 21.6 %reshape.112 = f32[28,64,32,64]{3,2,1,0:T(8,128)} reshape(f32[1,1,1792,8,256]{4,3,2,1,0:T(8,128)} %bitcast.47) | data formatting | bytes 29360128 | tf_op jit(solution)/shard_map/convert_element_type | solution.py:44
  243.1 29.9 %add.64 = f32[28,64,32,64]{3,2,1,0:T(8,128)} add(f32[28,64,32,64]{3,2,1,0:T(8,128)} %mul.98, f32[28,64,32,64]{3,2,1,0:T(8,128)} %reshape.112) | non-fusion elementwise | flops 3670016 | bytes 44040192 | tf_op jit(solution)/shard_map/add | solution.py:42
  273.0 52.6 %fusion = f32[28,32,64,64]{2,3,1,0:T(8,128)} fusion(f32[28,64,32,64]{3,2,1,0:T(8,128)} %add.64, f32[64]{0:T(128)S(1)} %get-tuple-element.5, f32[64]{0:T(128)S(1)} %get-tuple-element.4), kind=kOutput, calls=%fused_computation.2 | convolution fusion | flops 2818584576 | bytes 29360640 | tf_op jit(solution)/shard_map/ui,piqj,vj->pquv/dot_general | solution.py:20
  325.6 29.6 %fusion.7 = f32[28,32,64,64]{3,2,1,0:T(8,128)} fusion(f32[28,32,64,64]{2,3,1,0:T(8,128)} %fusion, f32[64]{0:T(128)S(1)} %get-tuple-element.5, f32[64]{0:T(128)S(1)} %get-tuple-element.4), kind=kOutput, calls=%fused_computation.21 | convolution fusion | flops 2818584576 | bytes 29360640 | tf_op jit(solution)/shard_map/ui,piqj,vj->pquv/dot_general | solution.py:20
  355.3 24.7 %reshape.101 = f32[28,32,4096]{2,1,0:T(8,128)} reshape(f32[28,32,64,64]{3,2,1,0:T(8,128)} %fusion.7) | data formatting | bytes 29360128 | tf_op jit(solution)/shard_map/reshape | solution.py:48
  380.0 398.1 %gather_fusion = f32[28672]{0:T(1024)S(1)} fusion(f32[28,32,4096]{2,1,0:T(8,128)} %reshape.101, s32[28672]{0:T(1024)S(1)} %reshape.115), kind=kCustom, calls=%fused_computation | custom fusion | bytes 573440 | tf_op jit(solution)/shard_map/jit(take_along_axis)/gather | solution.py:50
  778.6 156.3 %scatter_custom_fusion = f32[3670016]{0:T(1024)} fusion(s32[28672]{0:T(1024)} %reshape.121, f32[28672]{0:T(1024)S(1)} %reshape.123, f32[]{:T(128)} %constant.15.clone.1), kind=kCustom, calls=%fused_computation.7 | custom fusion | flops 28672 | bytes 14680576
  934.9 22.2 %reshape.102 = f32[28,32,64,64]{3,2,1,0:T(8,128)} reshape(f32[3670016]{0:T(1024)} %scatter_custom_fusion) | data formatting | bytes 29360128 | tf_op jit(solution)/shard_map/reshape | solution.py:51
  957.1 34.3 %fusion.5 = f32[28,32,64,64]{2,3,1,0:T(8,128)} fusion(f32[28,32,64,64]{3,2,1,0:T(8,128)} %reshape.102, f32[64]{0:T(128)S(1)} %copy-done.7, f32[64]{0:T(128)S(1)} %copy-done.5), kind=kOutput, calls=%fused_computation.19 | convolution fusion | flops 2818584576 | bytes 29360640 | tf_op jit(solution)/shard_map/ui,pquv,vj->piqj/dot_general | solution.py:24
  991.3 29.2 %convolution_bitcast_fusion = f32[28,64,32,64]{3,1,2,0:T(8,128)S(1)} fusion(f32[28,32,64,64]{2,3,1,0:T(8,128)} %fusion.5, f32[64]{0:T(128)S(1)} %copy-done.7, f32[64]{0:T(128)S(1)} %copy-done.5), kind=kOutput, calls=%fused_computation.6 | convolution fusion | flops 2818584576 | bytes 29360640 | tf_op jit(solution)/shard_map/ui,pquv,vj->piqj/dot_general | solution.py:24
  1020.6 19.3 %copy.33 = f32[28,64,32,64]{3,2,1,0:T(8,128)} copy(f32[28,64,32,64]{3,1,2,0:T(8,128)S(1)} %convolution_bitcast_fusion) | data formatting | bytes 29360128 | tf_op jit(solution)/shard_map/ui,pquv,vj->piqj/transpose | solution.py:24
  1039.9 25.4 %broadcast_in_dim.39 = f32[1,1792,2048]{2,1,0:T(8,128)} reshape(f32[28,64,32,64]{3,2,1,0:T(8,128)} %copy.33) | data formatting | bytes 29360128 | tf_op jit(solution)/shard_map/broadcast_in_dim | solution.py:55
  1065.3 494.5 %all-reduce.2.cloned.1.call-done = f32[1,1792,2048]{2,1,0:T(8,128)} async-done(((f32[1,1792,2048]{2,1,0:T(8,128)}), f32[1,1792,2048]{2,1,0:T(8,128)}) %all-reduce.2.cloned.1.call-update) | async-done | bytes 14680080 | tf_op jit(solution)/shard_map/psum | solution.py:54
  1559.7 32.1 %copy.35 = f32[1,1792,2048]{1,0,2:T(1,128)} copy(f32[1,1792,2048]{2,1,0:T(8,128)} %all-reduce.2.cloned.1.call-done) | data formatting | bytes 29360128 | tf_op jit(solution)/shard_map/psum | solution.py:54
  1591.8 5.6 all-to-all-start.1
  1597.4 25.4 %reshape.103 = f32[1,1,1792,2048]{3,2,1,0:T(8,128)} reshape(f32[28,64,32,64]{3,2,1,0:T(8,128)} %copy.33) | data formatting | bytes 29360128 | tf_op jit(solution)/shard_map/reshape | solution.py:52
  1622.8 15.8 reshape.111
  1638.6 20.9 %add_subtract_fusion = f32[1,1,1792,2048]{3,2,1,0:T(8,128)} fusion(f32[1,1,1792,2048]{3,2,1,0:T(8,128)} %reshape.103, f32[1,1,1792,2048]{3,2,1,0:T(8,128)} %reshape.111, f32[1,1,1792,2048]{3,2,1,0:T(8,128)} %param.4), kind=kLoop, calls=%fused_computation.5 | loop fusion | flops 11010048 | bytes 58720256 | tf_op jit(solution)/shard_map/sub | solution.py:53
  1659.6 99.3 %all-to-all-done.1 = f32[1,1792,2048]{1,0,2:T(1,128)} async-done(((f32[1,1792,2048]{1,0,2:T(1,128)}), f32[1,1792,2048]{1,0,2:T(1,128)}, u32[]{:S(2)}, u32[]{:S(2)}) %all-to-all-start.1) | async-done | bytes 14680096 | tf_op jit(solution)/shard_map/all_to_all | solution.py:55
  1758.9 11.3 copy.41
  1770.2 14.4 copy.36
  (34 shorter events, 3.1 us)
Async XLA Ops:
  7.2 103.7 %copy-start = (s32[28,32,4,32]{3,2,1,0:T(4,128)S(1)}, s32[28,32,4,32]{3,2,1,0:T(4,128)}, u32[]{:S(2)}) copy-start(s32[28,32,4,32]{3,2,1,0:T(4,128)} %param.5) | copy-start | bytes 1376260
  96.0 16.4 copy-start.9
  96.0 16.6 copy-start.8
  105.1 88.4 %all-to-all-start = ((bf16[8,2,229376]{2,1,0:T(2,128)(2,1)}), bf16[8,2,229376]{2,1,0:T(2,128)(2,1)}, u32[]{:S(2)}, u32[]{:S(2)}) async-start(bf16[8,2,229376]{2,1,0:T(2,128)(2,1)} %reshape.130), calls=%async_computation | async-start | bytes 14680064 | tf_op jit(solution)/shard_map/all_to_all | solution.py:39
  110.3 1449.5 %all-reduce.2.cloned.1.call-start = ((), (), s32[]{:S(2)}) async-start(), calls=%async_computation.2 | async-start | bytes 29360128 | tf_op jit(solution)/shard_map/psum | solution.py:54
  111.3 0.8 copy-start.2
  152.5 173.1 %copy-start.4 = (f32[64]{0:T(128)}, f32[64]{0:T(128)S(1)}, u32[]{:S(2)}) copy-start(f32[64]{0:T(128)S(1)} %get-tuple-element.4) | copy-start | bytes 772
  152.5 173.1 %copy-start.6 = (f32[64]{0:T(128)}, f32[64]{0:T(128)S(1)}, u32[]{:S(2)}) copy-start(f32[64]{0:T(128)S(1)} %get-tuple-element.5) | copy-start | bytes 772
  380.0 398.3 %copy-start.3 = (s32[28,32,1,32]{3,2,1,0:T(1,128)S(1)}, s32[28,32,1,32]{3,2,1,0:T(1,128)}, u32[]{:S(2)}) copy-start(s32[28,32,1,32]{3,2,1,0:T(1,128)} %copy-done.2) | copy-start | bytes 344068
  934.9 22.2 %copy-start.5 = (f32[64]{0:T(128)S(1)}, f32[64]{0:T(128)}, u32[]{:S(2)}) copy-start(f32[64]{0:T(128)} %copy-done.4) | copy-start | bytes 772
  934.9 22.2 %copy-start.7 = (f32[64]{0:T(128)S(1)}, f32[64]{0:T(128)}, u32[]{:S(2)}) copy-start(f32[64]{0:T(128)} %copy-done.6) | copy-start | bytes 772
  1591.8 167.0 %all-to-all-start.1 = ((f32[1,1792,2048]{1,0,2:T(1,128)}), f32[1,1792,2048]{1,0,2:T(1,128)}, u32[]{:S(2)}, u32[]{:S(2)}) async-start(f32[1,1792,2048]{1,0,2:T(1,128)} %copy.35), calls=%async_computation.1 | async-start | bytes 29360128 | tf_op jit(solution)/shard_map/all_to_all | solution.py:55
  1770.2 14.4 copy-start.1
Sparse Core Ops, SparseCore 0:
  1065.4 494.3 all-reduce.1
where the time goes:
time: 1810 us; the launch traced here: 1790 us
  local copies, waits for them, and re-layouts  689 us (38%)
  waiting for transfers between devices  635 us (35%)
  other arithmetic  297 us (16%)
  matrix products  146 us (8%)
    psum x1, waiting for transfers between devices, on_device(): total = lax.psum(restored, 'dp')  494 us
    gather x2, local copies, waits for them, and re-layouts, on_device(): values = jnp.take_along_axis(coeffs, own, axis=2)  398 us
    unnamed x5, other arithmetic  231 us
    all_to_all x1, waiting for transfers between devices, on_device(): lax.all_to_all(total[None], 'expert', split_axis=2, concat_axis=1, tiled=...  99.3 us
    dot_general x2, matrix products, forward(): jnp.einsum('ui,piqj,vj->pquv', cosine, blocks, cosine, precision=HIGHEST_...  82.3 us
    dot_general x2, matrix products, inverse(): jnp.einsum('ui,pquv,vj->piqj', cosine, coeffs, cosine, precision=HIGHEST_...  63.5 us
    convert_element_type x3, local copies, waits for them, and re-layouts, on_device(): decayed = MOMENTUM_DECAY * momentum.reshape(row_count, col_count) + shift...  53.4 us
    unnamed x26, local copies, waits for them, and re-layouts  48.5 us
  transfers between devices with their start and end apart: 3, of which 3 were waited for; matrix products, arithmetic and copies ran while one was open for 6% of the time, Pallas kernels for 0%

commit v1 on v0

--- a/solution.py
+++ b/solution.py
@@ -51,7 +51,8 @@
     selected = place(values, own, SPAN * SPAN).reshape(block_rows, block_cols, SPAN, SPAN)
     restored = inverse(selected, cosine).reshape(row_count, col_count)
     momentum_next = (decayed - restored).reshape(momentum.shape)
-    total = lax.psum(restored, "dp")
+    pieces = lax.all_gather(restored, "dp", axis=0, tiled=False)
+    total = pieces.sum(axis=0)
     update = lax.all_to_all(total[None], "expert", split_axis=2, concat_axis=1, tiled=True)
     return (momentum_next, update)
 

time: 1810 us -> 2320 us (1.28)
  waiting for transfers between devices: 635 us -> 1120 us
  other arithmetic: 297 us -> 321 us
    all_gather x0 -> x1, waiting for transfers between devices: none -> 975 us  [on_device(): pieces = lax.all_gather(restored, 'dp', axis=0, tiled=False)]
    psum x1 -> x0, waiting for transfers between devices: 494 us -> none  [on_device(): total = lax.psum(restored, 'dp')]
    psum x1 -> x0, local copies, waits for them, and re-layouts: 32.1 us -> none  [on_device(): total = lax.psum(restored, 'dp')]
    another operation x0 -> x1, local copies, waits for them, and re-layouts: none -> 25.4 us  [on_device(): pieces = lax.all_gather(restored, 'dp', axis=0, tiled=False)]
    reduce_sum x0 -> x1, other arithmetic: none -> 24.8 us  [on_device(): total = pieces.sum(axis=0)]
  transfers between devices with their start and end apart: 3 -> 3, of which waited for: 3 -> 3; matrix products, arithmetic and copies ran while one was open for 6% -> 4% of each run, Pallas kernels for 0% -> 0%
where the time goes in v1:
time: 2320 us; the launch traced here: 2300 us
  waiting for transfers between devices  1120 us (48%)
  local copies, waits for them, and re-layouts  689 us (30%)
  other arithmetic  321 us (14%)
  matrix products  146 us (6%)
    all_gather x1, waiting for transfers between devices, on_device(): pieces = lax.all_gather(restored, 'dp', axis=0, tiled=False)  975 us
    gather x2, local copies, waits for them, and re-layouts, on_device(): values = jnp.take_along_axis(coeffs, own, axis=2)  398 us
    unnamed x5, other arithmetic  231 us
    all_to_all x1, waiting for transfers between devices, on_device(): lax.all_to_all(total[None], 'expert', split_axis=2, concat_axis=1, tiled=...  99.3 us
    dot_general x2, matrix products, forward(): jnp.einsum('ui,piqj,vj->pquv', cosine, blocks, cosine, precision=HIGHEST_...  82.3 us
    dot_general x2, matrix products, inverse(): jnp.einsum('ui,pquv,vj->piqj', cosine, coeffs, cosine, precision=HIGHEST_...  63.5 us
    convert_element_type x3, local copies, waits for them, and re-layouts, on_device(): decayed = MOMENTUM_DECAY * momentum.reshape(row_count, col_count) + shift...  53.4 us
    unnamed x26, local copies, waits for them, and re-layouts  48.5 us
  transfers between devices with their start and end apart: 3, of which 3 were waited for; matrix products, arithmetic and copies ran while one was open for 4% of the time, Pallas kernels for 0%

profile of v1, /device:TPU:0, one launch (start us, length us, event | category | flops | bytes accessed | tf_op | source)
XLA Modules:
  0.0 2297.1 jit_solution(18206423486572765982)
XLA Ops:
  7.2 13.9 copy.44
  21.6 74.4 %reduce.4 = bf16[14336,256]{1,0:T(8,128)(2,1)} reduce(bf16[14336,1,1,256]{3,2,1,0:T(2,128)(2,1)} %bitcast.51, bf16[]{:T(256)} %broadcast.103), dimensions={1,2}, to_apply=%bitcast.47.reduce_sub_computation | reduce | bytes 14680066
  96.0 9.0 reshape.126
  105.1 5.2 all-to-all-start
  113.1 0.8 reshape.117
  113.9 14.1 broadcast_multiply_fusion
  128.0 24.3 %mul.98 = f32[28,64,32,64]{3,2,1,0:T(8,128)} reshape(f32[1,1,1792,2048]{3,2,1,0:T(8,128)} %broadcast_multiply_fusion) | data formatting | bytes 29360128 | tf_op jit(solution)/shard_map/mul | solution.py:42
  152.5 40.9 %all-to-all-done = bf16[8,2,229376]{2,1,0:T(2,128)(2,1)} async-done(((bf16[8,2,229376]{2,1,0:T(2,128)(2,1)}), bf16[8,2,229376]{2,1,0:T(2,128)(2,1)}, u32[]{:S(2)}, u32[]{:S(2)}) %all-to-all-start) | async-done | bytes 7340064 | tf_op jit(solution)/shard_map/all_to_all | solution.py:39
  193.4 12.1 reshape.127
  205.5 15.9 copy.43
  221.4 21.6 reshape.108
  243.1 29.9 %add.62 = f32[28,64,32,64]{3,2,1,0:T(8,128)} add(f32[28,64,32,64]{3,2,1,0:T(8,128)} %mul.98, f32[28,64,32,64]{3,2,1,0:T(8,128)} %reshape.108) | non-fusion elementwise | flops 3670016 | bytes 44040192 | tf_op jit(solution)/shard_map/add | solution.py:42
  273.0 52.6 %fusion = f32[28,32,64,64]{2,3,1,0:T(8,128)} fusion(f32[28,64,32,64]{3,2,1,0:T(8,128)} %add.62, f32[64]{0:T(128)S(1)} %get-tuple-element.5, f32[64]{0:T(128)S(1)} %get-tuple-element.4), kind=kOutput, calls=%fused_computation.2 | convolution fusion | flops 2818584576 | bytes 29360640 | tf_op jit(solution)/shard_map/ui,piqj,vj->pquv/dot_general | solution.py:20
  325.6 29.6 %fusion.7 = f32[28,32,64,64]{3,2,1,0:T(8,128)} fusion(f32[28,32,64,64]{2,3,1,0:T(8,128)} %fusion, f32[64]{0:T(128)S(1)} %get-tuple-element.5, f32[64]{0:T(128)S(1)} %get-tuple-element.4), kind=kOutput, calls=%fused_computation.21 | convolution fusion | flops 2818584576 | bytes 29360640 | tf_op jit(solution)/shard_map/ui,piqj,vj->pquv/dot_general | solution.py:20
  355.3 24.7 %reshape.99 = f32[28,32,4096]{2,1,0:T(8,128)} reshape(f32[28,32,64,64]{3,2,1,0:T(8,128)} %fusion.7) | data formatting | bytes 29360128 | tf_op jit(solution)/shard_map/reshape | solution.py:48
  380.0 398.3 %gather_fusion = f32[28672]{0:T(1024)S(1)} fusion(f32[28,32,4096]{2,1,0:T(8,128)} %reshape.99, s32[28672]{0:T(1024)S(1)} %reshape.111), kind=kCustom, calls=%fused_computation | custom fusion | bytes 573440 | tf_op jit(solution)/shard_map/jit(take_along_axis)/gather | solution.py:50
  778.8 156.3 %scatter_custom_fusion = f32[3670016]{0:T(1024)} fusion(s32[28672]{0:T(1024)} %reshape.117, f32[28672]{0:T(1024)S(1)} %reshape.119, f32[]{:T(128)} %constant.15.clone.1), kind=kCustom, calls=%fused_computation.7 | custom fusion | flops 28672 | bytes 14680576
  935.1 22.2 reshape.100
  957.3 34.3 %fusion.5 = f32[28,32,64,64]{2,3,1,0:T(8,128)} fusion(f32[28,32,64,64]{3,2,1,0:T(8,128)} %reshape.100, f32[64]{0:T(128)S(1)} %copy-done.7, f32[64]{0:T(128)S(1)} %copy-done.5), kind=kOutput, calls=%fused_computation.19 | convolution fusion | flops 2818584576 | bytes 29360640 | tf_op jit(solution)/shard_map/ui,pquv,vj->piqj/dot_general | solution.py:24
  991.5 29.2 %convolution_bitcast_fusion = f32[28,64,32,64]{3,1,2,0:T(8,128)S(1)} fusion(f32[28,32,64,64]{2,3,1,0:T(8,128)} %fusion.5, f32[64]{0:T(128)S(1)} %copy-done.7, f32[64]{0:T(128)S(1)} %copy-done.5), kind=kOutput, calls=%fused_computation.6 | convolution fusion | flops 2818584576 | bytes 29360640 | tf_op jit(solution)/shard_map/ui,pquv,vj->piqj/dot_general | solution.py:24
  1020.8 19.3 copy.30
  1040.1 25.4 %all_gather_reshape.3 = f32[1,1792,2048]{2,1,0:T(8,128)} reshape(f32[28,64,32,64]{3,2,1,0:T(8,128)} %copy.30) | data formatting | bytes 29360128 | tf_op jit(solution)/shard_map/all_gather;reshape | solution.py:54
  1065.5 975.1 %all-gather.2.cloned.1.call-done = f32[4,1792,2048]{2,1,0:T(8,128)} async-done(((f32[1,1792,2048]{2,1,0:T(8,128)}), f32[4,1792,2048]{2,1,0:T(8,128)}) %all-gather.2.cloned.1.call-update) | async-done | bytes 58720272 | tf_op jit(solution)/shard_map/all_gather | solution.py:54
  2040.5 24.8 %reduce_sum.9 = f32[1792,2048]{1,0:T(8,128)} reduce(f32[4,1792,2048]{2,1,0:T(8,128)} %all-gather.2.cloned.1.call-done, f32[]{:T(128)} %constant.15.clone.1), dimensions={0}, to_apply=%region_1.2 | reduce | flops 11010048 | bytes 73400320 | tf_op jit(solution)/shard_map/reduce_sum | solution.py:55
  2065.3 32.1 %copy.32 = f32[1,1792,2048]{1,0,2:T(1,128)} copy(f32[1,1792,2048]{2,1,0:T(8,128)} %bitcast.53) | data formatting | bytes 29360128 | tf_op jit(solution)/shard_map/broadcast_in_dim | solution.py:56
  2097.4 5.6 all-to-all-start.1
  2102.9 25.4 %reshape.101 = f32[1,1,1792,2048]{3,2,1,0:T(8,128)} reshape(f32[28,64,32,64]{3,2,1,0:T(8,128)} %copy.30) | data formatting | bytes 29360128 | tf_op jit(solution)/shard_map/reshape | solution.py:52
  2128.3 15.8 reshape.107
  2144.2 20.9 add_subtract_fusion
  2165.1 99.3 %all-to-all-done.1 = f32[1,1792,2048]{1,0,2:T(1,128)} async-done(((f32[1,1792,2048]{1,0,2:T(1,128)}), f32[1,1792,2048]{1,0,2:T(1,128)}, u32[]{:S(2)}, u32[]{:S(2)}) %all-to-all-start.1) | async-done | bytes 14680096 | tf_op jit(solution)/shard_map/all_to_all | solution.py:56
  2264.4 11.3 copy.38
  2275.7 14.4 copy.33
  (35 shorter events, 3.9 us)
Async XLA Ops:
  7.2 103.7 %copy-start = (s32[28,32,4,32]{3,2,1,0:T(4,128)S(1)}, s32[28,32,4,32]{3,2,1,0:T(4,128)}, u32[]{:S(2)}) copy-start(s32[28,32,4,32]{3,2,1,0:T(4,128)} %param.5) | copy-start | bytes 1376260
  96.0 16.4 copy-start.9
  96.0 16.6 copy-start.8
  105.1 88.4 %all-to-all-start = ((bf16[8,2,229376]{2,1,0:T(2,128)(2,1)}), bf16[8,2,229376]{2,1,0:T(2,128)(2,1)}, u32[]{:S(2)}, u32[]{:S(2)}) async-start(bf16[8,2,229376]{2,1,0:T(2,128)(2,1)} %reshape.126), calls=%async_computation | async-start | bytes 14680064 | tf_op jit(solution)/shard_map/all_to_all | solution.py:39
  110.3 1930.3 %all-gather.2.cloned.1.call-start = ((), (), s32[]{:S(2)}) async-start(), calls=%async_computation.2 | async-start | bytes 73400320 | tf_op jit(solution)/shard_map/all_gather | solution.py:54
  111.3 0.8 copy-start.2
  152.5 173.1 %copy-start.4 = (f32[64]{0:T(128)}, f32[64]{0:T(128)S(1)}, u32[]{:S(2)}) copy-start(f32[64]{0:T(128)S(1)} %get-tuple-element.4) | copy-start | bytes 772
  152.5 173.1 %copy-start.6 = (f32[64]{0:T(128)}, f32[64]{0:T(128)S(1)}, u32[]{:S(2)}) copy-start(f32[64]{0:T(128)S(1)} %get-tuple-element.5) | copy-start | bytes 772
  380.0 398.5 %copy-start.3 = (s32[28,32,1,32]{3,2,1,0:T(1,128)S(1)}, s32[28,32,1,32]{3,2,1,0:T(1,128)}, u32[]{:S(2)}) copy-start(s32[28,32,1,32]{3,2,1,0:T(1,128)} %copy-done.2) | copy-start | bytes 344068
  935.1 22.2 copy-start.5
  935.1 22.2 copy-start.7
  2097.4 167.0 %all-to-all-start.1 = ((f32[1,1792,2048]{1,0,2:T(1,128)}), f32[1,1792,2048]{1,0,2:T(1,128)}, u32[]{:S(2)}, u32[]{:S(2)}) async-start(f32[1,1792,2048]{1,0,2:T(1,128)} %copy.32), calls=%async_computation.1 | async-start | bytes 29360128 | tf_op jit(solution)/shard_map/all_to_all | solution.py:56
  2275.7 14.4 copy-start.1
Sparse Core Ops, SparseCore 0:
  1065.6 974.8 all-gather.1
